TPU v7x, 128 devices: a whole 4x4x4 slice. The times are simulated.
128 devices in a mesh: fsdp: 64 (over z, y, x), ep: 2 (over core).
Axes of the slice: x: 4, y: 4, z: 4, core: 2. Of those that a mesh axis runs over, the one named last changes fastest.
Arguments:
- x_in: bfloat16 [2, 131072, 512], P(None, ('fsdp', 'ep'))
- dy_out: bfloat16 [2, 131072, 512], P(None, ('fsdp', 'ep'))
- expert_idx: int32 [2, 131072, 2], P(None, ('fsdp', 'ep'))
- gate_prob: float32 [2, 131072, 2], P(None, ('fsdp', 'ep'))
- w_one: bfloat16 [8, 512, 1792], P('ep', 'fsdp')
- w_two: bfloat16 [8, 1792, 512], P('ep', None, 'fsdp')
- w_three: bfloat16 [8, 512, 1792], P('ep', 'fsdp')
Outputs:
- output 1: bfloat16 [2, 131072, 512], P(None, ('fsdp', 'ep'))
- output 2: float32 [2, 131072, 2], P(None, ('fsdp', 'ep'))
- output 3: float32 [8, 512, 1792], P('ep', 'fsdp')
- output 4: float32 [8, 1792, 512], P('ep', None, 'fsdp')
- output 5: float32 [8, 512, 1792], P('ep', 'fsdp')
All inputs are finite; a program needn't handle non-finite values.
Results may differ from a plain program's by a relative error of at most 0.00102.
Values are sent between devices in bfloat16 or wider.
A program may use at most 1 GiB of HBM per device.

v0:
```python
import jax
import jax.numpy as jnp
from jax import lax
from jax.sharding import PartitionSpec as P


def capacity_of(tok_rows, top_k, experts):
    return 8 * ((5 * tok_rows * top_k + 32 * experts - 1) // (32 * experts))


def route_tables(ids_flat, experts, capacity):
    n_choice = ids_flat.shape[0]
    one_hot = (ids_flat[:, None] == jnp.arange(experts, dtype=jnp.int32)[None, :]).astype(jnp.int32)
    position = jnp.sum((jnp.cumsum(one_hot, axis=0) - one_hot) * one_hot, axis=1)
    choice_slot = jnp.where(position < capacity, ids_flat * capacity + position, experts * capacity)
    holder = jnp.full((experts * capacity + 1,), n_choice, jnp.int32)
    holder = holder.at[choice_slot].set(jnp.arange(n_choice, dtype=jnp.int32))
    return choice_slot, holder[:experts * capacity]


def to_experts(send_buf):
    arrived = lax.all_to_all(send_buf, 'ep', 0, 2, tiled=True)
    return arrived.reshape(arrived.shape[1:])


def from_experts(row_block):
    arrived = lax.all_to_all(row_block[None], 'ep', 2, 0, tiled=True)
    return arrived.reshape((-1,) + arrived.shape[3:])


def expert_pass(x_rows, dy_rows, gate_rows, w_one, w_two, w_three):
    h_one = jnp.einsum('erd,edf->erf', x_rows, w_one, preferred_element_type=jnp.float32)
    h_three = jnp.einsum('erd,edf->erf', x_rows, w_three, preferred_element_type=jnp.float32)
    sigma_one = jax.nn.sigmoid(h_one)
    silu_one = h_one * sigma_one
    act_bf = (silu_one * h_three).astype(jnp.bfloat16)
    y_rows = jnp.einsum('erf,efd->erd', act_bf, w_two, preferred_element_type=jnp.float32)
    dg_rows = jnp.sum(dy_rows.astype(jnp.float32) * y_rows, axis=2)
    g_rows = (gate_rows[:, :, None] * dy_rows).astype(jnp.bfloat16)
    d_act = jnp.einsum('erd,efd->erf', g_rows, w_two, preferred_element_type=jnp.float32)
    dh_three = (d_act * silu_one).astype(jnp.bfloat16)
    dh_one = (d_act * h_three * sigma_one * (1.0 + h_one * (1.0 - sigma_one))).astype(jnp.bfloat16)
    dx_rows = (jnp.einsum('erf,edf->erd', dh_one, w_one, preferred_element_type=jnp.float32) + jnp.einsum('erf,edf->erd', dh_three, w_three, preferred_element_type=jnp.float32)).astype(jnp.bfloat16)
    gw_one = jnp.einsum('erd,erf->edf', x_rows, dh_one, preferred_element_type=jnp.float32)
    gw_two = jnp.einsum('erf,erd->efd', act_bf, g_rows, preferred_element_type=jnp.float32)
    gw_three = jnp.einsum('erd,erf->edf', x_rows, dh_three, preferred_element_type=jnp.float32)
    return dx_rows, dg_rows, (gw_one, gw_two, gw_three)


def solution(mesh):
    ep_size = mesh.shape['ep']
    tok_spec = P(None, ('fsdp', 'ep'), None)
    spec_edf = P('ep', 'fsdp', None)
    spec_efd = P('ep', None, 'fsdp')

    def local_step(x_in, dy_out, expert_idx, gate_prob, w_one, w_two, w_three):
        micro_count, tok_rows, d_model = x_in.shape
        top_k = expert_idx.shape[2]
        local_experts = w_one.shape[0]
        experts = local_experts * ep_size
        capacity = capacity_of(tok_rows, top_k, experts)
        n_choice = tok_rows * top_k
        full_one = lax.all_gather(w_one, 'fsdp', axis=1, tiled=True)
        full_two = lax.all_gather(w_two, 'fsdp', axis=2, tiled=True)
        full_three = lax.all_gather(w_three, 'fsdp', axis=1, tiled=True)
        zero_row = jnp.zeros((1, d_model), x_in.dtype)
        zero_val = jnp.zeros((1,), jnp.float32)
        send_shape = (ep_size, local_experts, capacity)
        dx_parts = []
        dg_parts = []
        grad_sum = None
        for mb_index in range(micro_count):
            choice_slot, holder = route_tables(expert_idx[mb_index].reshape(n_choice), experts, capacity)
            tok_slot = holder // top_k
            x_send = jnp.concatenate([x_in[mb_index], zero_row], axis=0)[tok_slot]
            dy_send = jnp.concatenate([dy_out[mb_index], zero_row], axis=0)[tok_slot]
            gate_send = jnp.concatenate([gate_prob[mb_index].reshape(n_choice), zero_val])[holder]
            x_rows = to_experts(x_send.reshape(send_shape + (d_model,)))
            dy_rows = to_experts(dy_send.reshape(send_shape + (d_model,)))
            gate_rows = to_experts(gate_send.reshape(send_shape))
            dx_rows, dg_rows, grad_part = expert_pass(x_rows, dy_rows, gate_rows, full_one, full_two, full_three)
            dx_back = jnp.concatenate([from_experts(dx_rows), zero_row], axis=0)
            dg_back = jnp.concatenate([from_experts(dg_rows), zero_val])
            picked = dx_back[choice_slot].reshape(tok_rows, top_k, d_model)
            dx_parts.append(jnp.sum(picked.astype(jnp.float32), axis=1).astype(jnp.bfloat16))
            dg_parts.append(dg_back[choice_slot].reshape(tok_rows, top_k))
            if grad_sum is None:
                grad_sum = grad_part
            else:
                grad_sum = tuple(prev_sum + new_part for prev_sum, new_part in zip(grad_sum, grad_part))
        dw_one = lax.psum_scatter(grad_sum[0], 'fsdp', scatter_dimension=1, tiled=True)
        dw_two = lax.psum_scatter(grad_sum[1], 'fsdp', scatter_dimension=2, tiled=True)
        dw_three = lax.psum_scatter(grad_sum[2], 'fsdp', scatter_dimension=1, tiled=True)
        return jnp.stack(dx_parts), jnp.stack(dg_parts), dw_one, dw_two, dw_three

    return jax.shard_map(local_step, mesh=mesh, in_specs=(tok_spec, tok_spec, tok_spec, tok_spec, spec_edf, spec_efd, spec_edf), out_specs=(tok_spec, tok_spec, spec_edf, spec_efd, spec_edf), check_vma=False)
```

profile of v0, /device:TPU:0, one launch (start us, length us, event | category | flops | bytes accessed | tf_op | source)
XLA Modules:
  0.0 1512.4 jit_solution(903370782608362222)
XLA Ops:
  25.8 8.2 gather_fusion.6
  39.7 13.6 gather_fusion.4
  61.9 8.2 gather_fusion.5
  94.6 13.6 gather_fusion
  115.1 8.2 gather_fusion.1
  146.4 12.4 fusion.24
  158.8 9.5 all-gather.4.cloned.1.call-done
  168.3 15.9 %fusion.5 = f32[4,640,1792]{2,1,0:T(8,128)} fusion(bf16[4,1792,512]{1,2,0:T(8,128)(2,1)} %all-gather.4.cloned.1.call-done, f32[4,640,512]{2,1,0:T(8,128)} %bitcast.140, f32[4,640]{1,0:T(4,128)S(1)} %mul.103), kind=kOutput, calls=%fused_computation.41 | convolution fusion | flops 4700241920 | bytes 30943232 | tf_op jit(solution)/shard_map/erd,efd->erf/dot_general | solution.py:40
  184.2 62.8 %all-gather.6.cloned.1.call-done = bf16[4,512,1792]{2,1,0:T(8,128)(2,1)} async-done(((bf16[4,8,1792]{2,1,0:T(8,128)(2,1)}), bf16[4,512,1792]{2,1,0:T(8,128)(2,1)}) %all-gather.6.cloned.1.call-update) | async-done | bytes 7340048 | tf_op jit(solution)/shard_map/all_gather | solution.py:65
  247.0 26.0 %multiply_convert_fusion.1 = (bf16[4,640,1792]{2,1,0:T(8,128)(2,1)}, bf16[4,640,1792]{2,1,0:T(8,128)(2,1)}, bf16[4,640,1792]{2,1,0:T(8,128)(2,1)}) fusion(f32[4,640,1792]{2,1,0:T(8,128)} %fusion.24, f32[4,640,1792]{2,1,0:T(8,128)} %fusion.5, bf16[4,640,512]{2,1,0:T(8,128)(2,1)S(1)} %bitcast.155, bf16[4,512,1792]{2,1,0:T(8,128)(2,1)} %all-gather.6.cloned.1.call-done), kind=kOutput, calls=%fused_computation.13 | convolution fusion | flops 4766433280 | bytes 74186752 | tf_op jit(solution)/shard_map/erd,edf->erf/dot_general | solution.py:33
  273.0 13.3 fusion.28
  286.3 12.2 fusion.26
  298.5 12.0 fusion.6
  310.4 26.0 %multiply_convert_fusion = (bf16[4,640,1792]{2,1,0:T(8,128)(2,1)}, bf16[4,640,1792]{2,1,0:T(8,128)(2,1)}, bf16[4,640,1792]{2,1,0:T(8,128)(2,1)}) fusion(f32[4,640,1792]{2,1,0:T(8,128)} %fusion.26, f32[4,640,1792]{2,1,0:T(8,128)} %fusion.6, bf16[4,640,512]{2,1,0:T(8,128)(2,1)S(1)} %bitcast.149, bf16[4,512,1792]{2,1,0:T(8,128)(2,1)} %all-gather.6.cloned.1.call-done), kind=kOutput, calls=%fused_computation.12 | convolution fusion | flops 4766433280 | bytes 74186752 | tf_op jit(solution)/shard_map/erd,edf->erf/dot_general | solution.py:33
  336.4 14.9 convolution_add_fusion.2
  351.3 13.9 fusion.4
  365.3 15.9 %convolution_add_fusion.1 = f32[4,1792,512]{1,2,0:T(8,128)} fusion(f32[4,1792,512]{1,2,0:T(8,128)} %fusion.4, bf16[4,640,1792]{2,1,0:T(8,128)(2,1)} %get-tuple-element.18, f32[4,640,512]{2,1,0:T(8,128)} %bitcast.143, f32[4,640]{1,0:T(4,128)S(1)} %mul.115), kind=kOutput, calls=%fused_computation.23 | convolution fusion | flops 4703911936 | bytes 43788288 | tf_op jit(solution)/shard_map/erf,erd->efd/dot_general | solution.py:45
  381.2 13.4 fusion.29
  394.6 14.9 convolution_add_fusion
  421.8 13.0 fusion.27
  434.8 12.2 fusion.3
  455.7 9.2 gather_fusion.7
  474.4 13.1 fusion.25
  487.5 12.1 fusion.2
  508.5 9.2 gather_fusion.3
  526.1 11.5 multiply_reduce_fusion
  545.1 12.0 gather_fusion.9
  557.8 11.5 multiply_reduce_fusion.1
  576.5 11.8 gather_fusion.8
  591.1 146.2 %reduce-scatter.4.cloned.1.call-done = f32[4,8,1792]{2,1,0:T(8,128)} async-done(((f32[4,512,1792]{2,1,0:T(8,128)}), f32[4,8,1792]{2,1,0:T(8,128)}) %reduce-scatter.4.cloned.1.call-update) | async-done | bytes 229392 | tf_op jit(solution)/shard_map/reduce_scatter | solution.py:91
  737.3 382.2 %reduce-scatter.6.cloned.1.call-done = f32[4,1792,8]{1,2,0:T(8,128)} async-done(((f32[4,1792,512]{1,2,0:T(8,128)}), f32[4,1792,8]{1,2,0:T(8,128)}) %reduce-scatter.6.cloned.1.call-update) | async-done | bytes 229392 | tf_op jit(solution)/shard_map/reduce_scatter | solution.py:92
  1119.5 385.7 %reduce-scatter.8.cloned.1.call-done = f32[4,8,1792]{2,1,0:T(8,128)} async-done(((f32[4,512,1792]{2,1,0:T(8,128)}), f32[4,8,1792]{2,1,0:T(8,128)}) %reduce-scatter.8.cloned.1.call-update) | async-done | bytes 229392 | tf_op jit(solution)/shard_map/reduce_scatter | solution.py:93
  (149 shorter events, 152.7 us)
Async XLA Ops:
  7.2 139.2 %all-gather.8.cloned.1.call-start = ((), (), s32[]{:S(2)}) async-start(), calls=%async_computation.15 | async-start | bytes 7454720 | tf_op jit(solution)/shard_map/all_gather | solution.py:63
  7.9 160.4 %all-gather.4.cloned.1.call-start = ((), (), s32[]{:S(2)}) async-start(), calls=%async_computation.13 | async-start | bytes 7454720 | tf_op jit(solution)/shard_map/all_gather | solution.py:64
  8.6 238.3 %all-gather.6.cloned.1.call-start = ((), (), s32[]{:S(2)}) async-start(), calls=%async_computation.14 | async-start | bytes 7454720 | tf_op jit(solution)/shard_map/all_gather | solution.py:65
  17.1 0.6 copy-start.5
  25.8 12.8 copy-start.9
  34.0 20.0 %all-to-all-start.6 = ((bf16[2,4,320,512]{3,2,1,0:T(8,128)(2,1)}), bf16[2,4,320,512]{3,2,1,0:T(8,128)(2,1)S(1)}, u32[]{:S(2)}, u32[]{:S(2)}) async-start(bf16[2,4,320,512]{3,2,1,0:T(8,128)(2,1)} %bitcast.157), calls=%async_computation.6 | async-start | bytes 5242880 | tf_op jit(solution)/shard_map/all_to_all | solution.py:22
  54.0 36.6 %all-to-all-start.4 = ((f32[2,4,320]{2,1,0:T(4,128)}), f32[2,4,320]{2,1,0:T(4,128)S(1)}, u32[]{:S(2)}, u32[]{:S(2)}) async-start(f32[2,4,320]{2,1,0:T(4,128)} %reshape.184), calls=%async_computation.4 | async-start | bytes 24576 | tf_op jit(solution)/shard_map/all_to_all | solution.py:22
  61.9 8.2 copy-start.3
  73.7 0.6 copy-start.7
  90.6 18.3 %all-to-all-start.2 = ((bf16[2,4,320,512]{3,2,1,0:T(8,128)(2,1)}), bf16[2,4,320,512]{3,2,1,0:T(8,128)(2,1)S(1)}, u32[]{:S(2)}, u32[]{:S(2)}) async-start(bf16[2,4,320,512]{3,2,1,0:T(8,128)(2,1)} %bitcast.159), calls=%async_computation.2 | async-start | bytes 5242880 | tf_op jit(solution)/shard_map/all_to_all | solution.py:22
  108.9 14.4 all-to-all-start
  123.3 6.9 all-to-all-start.5
  130.2 1.5 copy-start.2
  131.7 10.0 all-to-all-start.1
  136.7 9.7 copy-start.1
  136.7 600.6 %reduce-scatter.4.cloned.1.call-start = ((), (), s32[]{:S(2)}) async-start(), calls=%async_computation.16 | async-start | bytes 14909440 | tf_op jit(solution)/shard_map/reduce_scatter | solution.py:91
  273.0 13.3 copy-start
  273.0 25.5 %slice-start = ((s8[5242880]{0:T(1024)(128)(4,1)}), s8[4194304]{0:T(1024)(128)(4,1)S(1)}, s32[]{:S(2)}) async-start(s8[5242880]{0:T(1024)(128)(4,1)} %bitcast.145), calls=%async_computation.19 | async-start | bytes 8388608
  286.3 12.2 slice-start.1
  351.3 768.2 %reduce-scatter.6.cloned.1.call-start = ((), (), s32[]{:S(2)}) async-start(), calls=%async_computation.17 | async-start | bytes 14909440 | tf_op jit(solution)/shard_map/reduce_scatter | solution.py:92
  381.2 1124.0 %reduce-scatter.8.cloned.1.call-start = ((), (), s32[]{:S(2)}) async-start(), calls=%async_computation.18 | async-start | bytes 14909440 | tf_op jit(solution)/shard_map/reduce_scatter | solution.py:93
  415.4 6.3 copy-start.6
  415.4 6.4 copy-start.8
  569.4 20.2 %copy-start.4 = (bf16[1024,512]{1,0:T(8,128)(2,1)S(1)}, bf16[1024,512]{1,0:T(8,128)(2,1)}, u32[]{:S(2)}) copy-start(bf16[1024,512]{1,0:T(8,128)(2,1)} %reduce_sum.69) | copy-start | bytes 3145732
Sparse Core Ops, SparseCore 0:
  10.9 78.7 all-gather.7
  92.5 75.7 all-gather.3
  171.2 75.7 all-gather.5
  351.4 385.8 reduce-scatter.3
  740.1 379.2 reduce-scatter.5
  1122.3 382.8 reduce-scatter.7
where the time goes:
time: 1520 us; the launch traced here: 1510 us
  waiting for transfers between devices  991 us (65%)
  matrix products  264 us (17%)
  local copies, waits for them, and re-layouts  165 us (11%)
  other arithmetic  34.4 us (2%)
  starting transfers between devices  23.3 us (2%)
  blocking collectives  19.1 us (1%)
    reduce_scatter x1, waiting for transfers between devices, local_step(): lax.psum_scatter(grad_sum[2], 'fsdp', scatter_dimension=1, tiled=True)  386 us
    reduce_scatter x1, waiting for transfers between devices, local_step(): lax.psum_scatter(grad_sum[1], 'fsdp', scatter_dimension=2, tiled=True)  382 us
    reduce_scatter x1, waiting for transfers between devices, local_step(): lax.psum_scatter(grad_sum[0], 'fsdp', scatter_dimension=1, tiled=True)  146 us
    all_gather x1, waiting for transfers between devices, local_step(): full_three = lax.all_gather(w_three, 'fsdp', axis=1, tiled=True)  62.8 us
    dot_general x2, matrix products, expert_pass(): jnp.einsum('erd,edf->erf', x_rows, w_three, preferred_element_type=jnp.fl...  52 us
  transfers between devices with their start and end apart: 12, of which 6 were waited for; matrix products, arithmetic and copies ran while one was open for 24% of the time, Pallas kernels for 0%

commit v1 on v0

v1 whole, which is shorter than its diff:
```python
import functools

import jax
import jax.numpy as jnp
from jax import lax
from jax.experimental import pallas as pl
from jax.experimental.pallas import tpu as pltpu
from jax.sharding import Mesh, PartitionSpec as P

F32 = jnp.float32
BF16 = jnp.bfloat16
ROW_TILE = 512
COL_TILE = 256


def capacity_of(tok_rows, top_k, experts):
    return 8 * ((5 * tok_rows * top_k + 32 * experts - 1) // (32 * experts))


def route_tables(ids_flat, experts, capacity):
    n_choice = ids_flat.shape[0]
    one_hot = (ids_flat[:, None] == jnp.arange(experts, dtype=jnp.int32)[None, :]).astype(jnp.int32)
    position = jnp.sum((jnp.cumsum(one_hot, axis=0) - one_hot) * one_hot, axis=1)
    choice_slot = jnp.where(position < capacity, ids_flat * capacity + position, experts * capacity)
    holder = jnp.full((experts * capacity + 1,), n_choice, jnp.int32)
    holder = holder.at[choice_slot].set(jnp.arange(n_choice, dtype=jnp.int32))
    return choice_slot, holder[:experts * capacity]


def expert_kernel(ff, first, x_ref, dy_ref, q_ref, w_hbm, wt_hbm, *rest):
    if first:
        dx_ref, dg_ref, gw_hbm, w_v, wt_v, gw_v, xt_v, gt_v, sems = rest
        gin_hbm = None
    else:
        gin_hbm, dx_ref, dg_ref, gw_hbm, w_v, wt_v, gw_v, xt_v, gt_v, sems = rest
    step = pl.program_id(0)

    @pl.when(step == 0)
    def _():
        copies = [pltpu.make_async_copy(w_hbm, w_v, sems.at[0]), pltpu.make_async_copy(wt_hbm, wt_v, sems.at[1])]
        if not first:
            copies.append(pltpu.make_async_copy(gin_hbm, gw_v, sems.at[2]))
        for copy in copies:
            copy.start()
        if first:
            gw_v[...] = jnp.zeros_like(gw_v)
        for copy in copies:
            copy.wait()

    x = x_ref[...]
    dyf = dy_ref[...].astype(F32)
    g = (q_ref[...] * dyf).astype(BF16)
    xt_v[...] = x.T
    gt_v[...] = g.T
    dot = functools.partial(jnp.dot, preferred_element_type=F32)
    y = None
    dx = None
    for lo in range(0, ff, COL_TILE):
        one, two, three = (pl.ds(k * ff + lo, COL_TILE) for k in range(3))
        h_one = dot(x, w_v[:, one])
        h_three = dot(x, w_v[:, three])
        d_act = dot(g, w_v[:, two])
        sigma = jax.nn.sigmoid(h_one)
        silu = h_one * sigma
        act = (silu * h_three).astype(BF16)
        dh_three = (d_act * silu).astype(BF16)
        dh_one = (d_act * h_three * sigma * (1.0 + h_one * (1.0 - sigma))).astype(BF16)
        y_part = dot(act, wt_v[two, :])
        dx_part = dot(dh_one, wt_v[one, :]) + dot(dh_three, wt_v[three, :])
        y = y_part if y is None else y + y_part
        dx = dx_part if dx is None else dx + dx_part
        gw_v[:, one] += dot(xt_v[...], dh_one)
        gw_v[:, three] += dot(xt_v[...], dh_three)
        gw_v[:, two] += dot(gt_v[...], act)
    dg_ref[...] = jnp.sum(dyf * y, axis=1, keepdims=True)
    dx_ref[...] = dx.astype(BF16)

    @pl.when(step == pl.num_programs(0) - 1)
    def _():
        out = pltpu.make_async_copy(gw_v, gw_hbm, sems.at[0])
        out.start()
        out.wait()


def expert_pass(x_rows, dy_rows, gate_rows, w_full, wt_full, grad_in):
    rows, d_model = x_rows.shape
    ff = w_full.shape[1] // 3
    first = grad_in is None
    row_block = pl.BlockSpec((ROW_TILE, d_model), lambda i: (i, 0))
    col_block = pl.BlockSpec((ROW_TILE, 1), lambda i: (i, 0))
    whole = pl.BlockSpec(memory_space=pl.ANY)
    args = [x_rows, dy_rows, gate_rows, w_full, wt_full] + ([] if first else [grad_in])
    in_specs = [row_block, row_block, col_block, whole, whole] + ([] if first else [whole])
    return pl.pallas_call(
        functools.partial(expert_kernel, ff, first),
        grid=(rows // ROW_TILE,),
        in_specs=in_specs,
        out_specs=[row_block, col_block, whole],
        out_shape=[
            jax.ShapeDtypeStruct((rows, d_model), BF16),
            jax.ShapeDtypeStruct((rows, 1), F32),
            jax.ShapeDtypeStruct((d_model, 3 * ff), F32),
        ],
        scratch_shapes=[
            pltpu.VMEM((d_model, 3 * ff), BF16),
            pltpu.VMEM((3 * ff, d_model), BF16),
            pltpu.VMEM((d_model, 3 * ff), F32),
            pltpu.VMEM((d_model, ROW_TILE), BF16),
            pltpu.VMEM((d_model, ROW_TILE), BF16),
            pltpu.SemaphoreType.DMA((3,)),
        ],
        compiler_params=pltpu.CompilerParams(vmem_limit_bytes=60 * 2**20),
        cost_estimate=pl.CostEstimate(flops=18 * rows * d_model * ff, bytes_accessed=40 * 2**20, transcendentals=2 * rows * ff),
        name='expert_first' if first else 'expert_next',
    )(*args)


def solution(mesh):
    side = round(mesh.shape['fsdp'] ** (1 / 3))
    cores = mesh.shape['ep']
    grid_mesh = Mesh(mesh.devices.reshape(side, side, side, cores), ('z', 'y', 'x', 'c'))
    tok_spec = P(None, ('z', 'y', 'x', 'c'), None)
    spec_edf = P('c', ('z', 'y', 'x'), None)
    spec_efd = P('c', None, ('z', 'y', 'x'))
    ring = ('x', 'c')

    def local_step(x_in, dy_out, expert_idx, gate_prob, w_one, w_two, w_three):
        micro_count, tok_rows, d_model = x_in.shape
        top_k = expert_idx.shape[2]
        local_experts, shard, ff = w_one.shape
        experts = local_experts * cores
        capacity = capacity_of(tok_rows, top_k, experts)
        n_choice = tok_rows * top_k
        rows = experts * capacity
        w_cat = jnp.concatenate([w_one, jnp.transpose(w_two, (0, 2, 1)), w_three], axis=2)
        w_mine = lax.all_to_all(w_cat, 'x', 0, 0, tiled=True).reshape(local_experts * shard, 3 * ff)
        w_full = lax.all_gather(w_mine, ('z', 'y'), axis=0, tiled=True)
        wt_full = w_full.T
        zero_row = jnp.zeros((1, d_model), x_in.dtype)
        zero_val = jnp.zeros((1,), F32)
        send_shape = (experts, capacity)
        sent = []
        for mb_index in range(micro_count):
            ids = expert_idx[mb_index].reshape(n_choice)
            owner = (ids % local_experts) * cores + ids // local_experts
            choice_slot, holder = route_tables(owner, experts, capacity)
            tok_slot = holder // top_k
            x_send = jnp.concatenate([x_in[mb_index], zero_row], axis=0)[tok_slot]
            dy_send = jnp.concatenate([dy_out[mb_index], zero_row], axis=0)[tok_slot]
            gate_send = jnp.concatenate([gate_prob[mb_index].reshape(n_choice), zero_val])[holder]
            x_rows = lax.all_to_all(x_send.reshape(send_shape + (d_model,)), ring, 0, 0, tiled=True)
            dy_rows = lax.all_to_all(dy_send.reshape(send_shape + (d_model,)), ring, 0, 0, tiled=True)
            gate_rows = lax.all_to_all(gate_send.reshape(send_shape), ring, 0, 0, tiled=True)
            sent.append((choice_slot, x_rows, dy_rows, gate_rows))
        dx_parts = []
        dg_parts = []
        grad_sum = None
        for choice_slot, x_rows, dy_rows, gate_rows in sent:
            dx_rows, dg_rows, grad_sum = expert_pass(x_rows.reshape(rows, d_model), dy_rows.reshape(rows, d_model), gate_rows.reshape(rows, 1), w_full, wt_full, grad_sum)
            dx_back = lax.all_to_all(dx_rows.reshape(send_shape + (d_model,)), ring, 0, 0, tiled=True).reshape(rows, d_model)
            dg_back = lax.all_to_all(dg_rows.reshape(send_shape), ring, 0, 0, tiled=True).reshape(rows)
            picked = jnp.concatenate([dx_back, zero_row], axis=0)[choice_slot].reshape(tok_rows, top_k, d_model)
            dx_parts.append(jnp.sum(picked.astype(F32), axis=1).astype(BF16))
            dg_parts.append(jnp.concatenate([dg_back, zero_val])[choice_slot].reshape(tok_rows, top_k))
        dw_mine = lax.psum_scatter(grad_sum, ('z', 'y'), scatter_dimension=0, tiled=True)
        dw_all = lax.all_to_all(dw_mine.reshape(local_experts, shard, 3 * ff), 'x', 0, 0, tiled=True)
        dw_one, dw_two, dw_three = dw_all[:, :, :ff], jnp.transpose(dw_all[:, :, ff:2 * ff], (0, 2, 1)), dw_all[:, :, 2 * ff:]
        return jnp.stack(dx_parts), jnp.stack(dg_parts), dw_one, dw_two, dw_three

    return jax.shard_map(local_step, mesh=grid_mesh, in_specs=(tok_spec, tok_spec, tok_spec, tok_spec, spec_edf, spec_efd, spec_edf), out_specs=(tok_spec, tok_spec, spec_edf, spec_efd, spec_edf), check_vma=False)
```

time: 1520 us -> 515 us (0.34)
  waiting for transfers between devices: 991 us -> 97.4 us
  matrix products: 264 us -> 0 us
  Pallas kernels: 0 us -> 121 us
  blocking collectives: 19.1 us -> 43.7 us
  starting transfers between devices: 23.3 us -> 43.6 us
    reduce_scatter x3 -> x1, waiting for transfers between devices: 914 us -> 1.53 us  [local_step(): lax.psum_scatter(grad_sum, ('z', 'y'), scatter_dimension=0, tiled=True)]
    dot_general x18 -> x0, matrix products: 264 us -> none  [the longest x2 52 us: expert_pass(): jnp.einsum('erd,edf->erf', x_rows, w_three, preferred_element_type=jnp.fl...]
    pallas_call x0 -> x2, Pallas kernels: none -> 121 us  [expert_pass(): pl.pallas_call(functools.partial(expert_kernel, ff, first), grid=(rows //...]
    all_to_all x6 -> x10, waiting for transfers between devices: 2.92 us -> 95.9 us  [the longest x2 47.3 us: local_step(): lax.all_to_all(x_send.reshape(send_shape + (d_model,)), ring, 0, 0, tiled...]
    all_gather x3 -> x1, waiting for transfers between devices: 72.3 us -> 0.01 us  [local_step(): w_full = lax.all_gather(w_mine, ('z', 'y'), axis=0, tiled=True)]
    all_to_all x4 -> x2, blocking collectives: 19.1 us -> 43.7 us  [the longest x1 36 us: local_step(): lax.all_to_all(dx_rows.reshape(send_shape + (d_model,)), ring, 0, 0, tile...]
    all_to_all x6 -> x10, starting transfers between devices: 23 us -> 43.6 us  [the longest x2 9.21 us: local_step(): lax.all_to_all(x_send.reshape(send_shape + (d_model,)), ring, 0, 0, tiled...]
  transfers between devices with their start and end apart: 12 -> 12, of which waited for: 6 -> 7; matrix products, arithmetic and copies ran while one was open for 24% -> 35% of each run, Pallas kernels for 0% -> 12%
where the time goes in v1:
time: 515 us; the launch traced here: 506 us
  local copies, waits for them, and re-layouts  157 us (30%)
  Pallas kernels  121 us (23%)
  waiting for transfers between devices  97.4 us (19%)
  blocking collectives  43.7 us (8%)
  starting transfers between devices  43.6 us (8%)
  other arithmetic  27.6 us (5%)
  between operations  14.9 us (3%)
    pallas_call x2, Pallas kernels, expert_pass(): pl.pallas_call(functools.partial(expert_kernel, ff, first), grid=(rows //...  121 us
    all_to_all x2, waiting for transfers between devices, local_step(): lax.all_to_all(x_send.reshape(send_shape + (d_model,)), ring, 0, 0, tiled...  47.3 us
    all_to_all x1, blocking collectives, local_step(): lax.all_to_all(dx_rows.reshape(send_shape + (d_model,)), ring, 0, 0, tile...  36 us
    all_to_all x1, waiting for transfers between devices, local_step(): lax.all_to_all(dx_rows.reshape(send_shape + (d_model,)), ring, 0, 0, tile...  32.7 us
    gather x2, local copies, waits for them, and re-layouts, local_step(): jnp.concatenate([gate_prob[mb_index].reshape(n_choice), zero_val])[holder]  27.2 us
    gather x2, local copies, waits for them, and re-layouts, local_step(): jnp.concatenate([dg_back, zero_val])[choice_slot].reshape(tok_rows, top_k)  23.6 us
    gather x2, local copies, waits for them, and re-layouts, local_step(): jnp.concatenate([dx_back, zero_row], axis=0)[choice_slot]  18.4 us
    gather x2, local copies, waits for them, and re-layouts, local_step(): x_send = jnp.concatenate([x_in[mb_index], zero_row], axis=0)[tok_slot]  16.4 us
  transfers between devices with their start and end apart: 12, of which 7 were waited for; matrix products, arithmetic and copies ran while one was open for 35% of the time, Pallas kernels for 12%

profile of v1, /device:TPU:0, one launch (start us, length us, event | category | flops | bytes accessed | tf_op | source)
XLA Modules:
  0.0 505.6 jit_solution(891843169646779835)
XLA Ops:
  8.9 4.4 all-to-all-start.3
  21.6 8.1 %scatter_custom_fusion = s32[2561]{0:T(1024)S(1)} fusion(s32[2048]{0:T(1024)S(1)} %bitcast.89, s32[2048]{0:T(1024)S(1)} %iota.19, s32[]{:T(128)} %constant.74.clone.1), kind=kCustom, calls=%fused_computation.132 | custom fusion | bytes 10248 | tf_op jit(solution)/shard_map/scatter | solution.py:26
  29.8 13.6 %gather_fusion.2 = f32[2560]{0:T(1024)S(1)} fusion(f32[2049]{0:T(1024)S(1)} %get-tuple-element.40, s32[3072]{0:T(1024)S(1)} %get-tuple-element.41), kind=kCustom, calls=%fused_computation.2 | custom fusion | bytes 30720 | tf_op jit(solution)/shard_map/gather | solution.py:150
  44.1 3.9 all-to-all-start.2
  52.1 8.1 %scatter_custom_fusion.1 = s32[2561]{0:T(1024)S(1)} fusion(s32[2048]{0:T(1024)S(1)} %bitcast.91, s32[2048]{0:T(1024)S(1)} %iota.20, s32[]{:T(128)} %constant.74.clone.1), kind=kCustom, calls=%fused_computation.130 | custom fusion | bytes 10248 | tf_op jit(solution)/shard_map/scatter | solution.py:26
  60.2 13.6 %gather_fusion.6 = f32[2560]{0:T(1024)S(1)} fusion(f32[2049]{0:T(1024)S(1)} %get-tuple-element.39, s32[3072]{0:T(1024)S(1)} %get-tuple-element.37), kind=kCustom, calls=%fused_computation.6 | custom fusion | bytes 30720 | tf_op jit(solution)/shard_map/gather | solution.py:150
  74.5 4.8 all-to-all-start.7
  81.0 8.2 %gather_fusion.4 = bf16[2560,512]{1,0:T(8,128)(2,1)} fusion(bf16[1025,512]{1,0:T(8,128)(2,1)S(1)} %concatenate.38, s32[3072]{0:T(1024)S(1)} %get-tuple-element.38), kind=kCustom, calls=%fused_computation.4 | custom fusion | bytes 5253120 | tf_op jit(solution)/shard_map/gather | solution.py:148
  89.3 4.8 all-to-all-start.5
  94.2 8.2 %gather_fusion = bf16[2560,512]{1,0:T(8,128)(2,1)} fusion(bf16[1025,512]{1,0:T(8,128)(2,1)S(1)} %concatenate.33, s32[3072]{0:T(1024)S(1)} %get-tuple-element.42), kind=kCustom, calls=%fused_computation | custom fusion | bytes 5253120 | tf_op jit(solution)/shard_map/gather | solution.py:148
  102.4 24.5 %all-to-all-done.5 = bf16[8,320,512]{2,1,0:T(8,128)(2,1)} async-done(((bf16[8,320,512]{2,1,0:T(8,128)(2,1)}), bf16[8,320,512]{2,1,0:T(8,128)(2,1)}, u32[]{:S(2)}, u32[]{:S(2)}) %all-to-all-start.5) | async-done | bytes 2621472 | tf_op jit(solution)/shard_map/all_to_all | solution.py:151
  126.9 4.4 all-to-all-start
  133.1 8.2 %gather_fusion.1 = bf16[2560,512]{1,0:T(8,128)(2,1)} fusion(bf16[1025,512]{1,0:T(8,128)(2,1)S(1)} %concatenate.34, s32[3072]{0:T(1024)S(1)} %get-tuple-element.42), kind=kCustom, calls=%fused_computation.1 | custom fusion | bytes 5253120 | tf_op jit(solution)/shard_map/gather | solution.py:149
  141.2 22.7 %all-to-all-done = bf16[8,320,512]{2,1,0:T(8,128)(2,1)} async-done(((bf16[8,320,512]{2,1,0:T(8,128)(2,1)}), bf16[8,320,512]{2,1,0:T(8,128)(2,1)}, u32[]{:S(2)}, u32[]{:S(2)}) %all-to-all-start) | async-done | bytes 2621472 | tf_op jit(solution)/shard_map/all_to_all | solution.py:151
  164.0 4.9 all-to-all-start.1
  168.9 8.2 %gather_fusion.5 = bf16[2560,512]{1,0:T(8,128)(2,1)} fusion(bf16[1025,512]{1,0:T(8,128)(2,1)S(1)} %concatenate.39, s32[3072]{0:T(1024)S(1)} %get-tuple-element.38), kind=kCustom, calls=%fused_computation.5 | custom fusion | bytes 5253120 | tf_op jit(solution)/shard_map/gather | solution.py:149
  181.6 8.3 %copy.33 = bf16[512,5376]{0,1:T(8,128)(2,1)} copy(bf16[512,5376]{1,0:T(8,128)(2,1)} %all-gather.2.cloned.1.call-done.w_hbm) | data formatting | bytes 11010048 | tf_op jit(solution)/shard_map/all_gather | solution.py:137
  189.9 11.6 %all-to-all-done.1 = bf16[8,320,512]{2,1,0:T(8,128)(2,1)} async-done(((bf16[8,320,512]{2,1,0:T(8,128)(2,1)}), bf16[8,320,512]{2,1,0:T(8,128)(2,1)}, u32[]{:S(2)}, u32[]{:S(2)}) %all-to-all-start.1) | async-done | bytes 2621472 | tf_op jit(solution)/shard_map/all_to_all | solution.py:152
  201.6 3.6 all-to-all-start.6
  205.2 59.1 %expert_first.1 = (bf16[2560,512]{1,0:T(8,128)(2,1)}, f32[2560,1]{1,0:T(8,128)}, f32[512,5376]{1,0:T(8,128)}) custom-call(bf16[2560,512]{1,0:T(8,128)(2,1)} %bitcast.5.x_ref, bf16[2560,512]{1,0:T(8,128)(2,1)} %bitcast.8.dy_ref, f32[2560,1]{1,0:T(8,128)} %reshape.542.q_ref, bf16[512,5376]{1,0:T(8,128)(2,1)} %all-gather.2.cloned.1.call-done.w_hbm, ...), custom_call_target="tpu_custom_call" | custom-call | flops 42278584320 | bytes 41943040 | tf_op jit(solution)/shard_map/expert_first/pallas_call | solution.py:94
  265.9 62.2 %expert_next.1 = (bf16[2560,512]{1,0:T(8,128)(2,1)}, f32[2560,1]{1,0:T(8,128)}, f32[512,5376]{1,0:T(8,128)}) custom-call(bf16[2560,512]{1,0:T(8,128)(2,1)} %bitcast.20.x_ref, bf16[2560,512]{1,0:T(8,128)(2,1)} %bitcast.83, f32[2560,1]{1,0:T(8,128)} %reshape.543.q_ref, bf16[512,5376]{1,0:T(8,128)(2,1)} %all-gather.2.cloned.1.call-done.w_hbm, ...), custom_call_target="tpu_custom_call" | custom-call | flops 42278584320 | bytes 41943040 | tf_op jit(solution)/shard_map/expert_next/pallas_call | solution.py:94
  330.7 4.7 all-to-all-start.10
  340.5 7.7 %all_to_all.78 = f32[8,1,320]{2,1,0:T(1,128)S(1)} all-to-all(f32[8,1,320]{2,1,0:T(1,128)S(1)} %all_to_all.64), channel_id=1, replica_groups=mesh['z'=4,'y'=4,'x'=4,'c'=2] {'x','c'}, dimensions={0} | all-to-all | bytes 20480 | tf_op jit(solution)/shard_map/all_to_all | solution.py:161
  348.2 36.0 %all_to_all.79 = bf16[8,320,512]{2,1,0:T(8,128)(2,1)} all-to-all(bf16[8,320,512]{2,1,0:T(8,128)(2,1)S(1)} %bitcast.82), channel_id=1, replica_groups=mesh['z'=4,'y'=4,'x'=4,'c'=2] {'x','c'}, dimensions={0} | all-to-all | bytes 5242880 | tf_op jit(solution)/shard_map/all_to_all | solution.py:160
  387.8 32.7 %all-to-all-done.4 = bf16[8,320,512]{2,1,0:T(8,128)(2,1)S(1)} async-done(((bf16[8,320,512]{2,1,0:T(8,128)(2,1)}), bf16[8,320,512]{2,1,0:T(8,128)(2,1)S(1)}, u32[]{:S(2)}, u32[]{:S(2)}) %all-to-all-start.4) | async-done | bytes 2621472 | tf_op jit(solution)/shard_map/all_to_all | solution.py:160
  422.0 4.5 all-to-all-start.11
  426.8 11.8 %gather_fusion.8 = f32[2048]{0:T(1024)S(1)} fusion(f32[2561]{0:T(1024)S(1)} %pad_maximum_fusion.5, s32[2048]{0:T(1024)S(1)} %broadcast_clamp_fusion.1), kind=kCustom, calls=%fused_computation.8 | custom fusion | bytes 24576 | tf_op jit(solution)/shard_map/gather | solution.py:164
  439.2 11.8 %gather_fusion.9 = f32[2048]{0:T(1024)S(1)} fusion(f32[2561]{0:T(1024)S(1)} %pad_maximum_fusion.4, s32[2048]{0:T(1024)S(1)} %broadcast_clamp_fusion), kind=kCustom, calls=%fused_computation.9 | custom fusion | bytes 24576 | tf_op jit(solution)/shard_map/gather | solution.py:164
  454.2 9.2 %gather_fusion.7 = bf16[2048,512]{1,0:T(8,128)(2,1)} fusion(bf16[2561,512]{1,0:T(8,128)(2,1)S(1)} %concatenate.41, s32[2048]{0:T(1024)S(1)} %broadcast_clamp_fusion), kind=kCustom, calls=%fused_computation.7 | custom fusion | bytes 4202496 | tf_op jit(solution)/shard_map/gather | solution.py:162
  466.2 6.6 %reduce_sum.51 = bf16[1024,512]{1,0:T(8,128)(2,1)} reduce(bf16[1024,2,512]{2,1,0:T(2,128)(2,1)S(1)} %reshape.436, bf16[]{:T(256)} %constant.73.clone.1), dimensions={1}, to_apply=%region_9.10 | reduce | flops 524288 | bytes 3145730 | tf_op jit(solution)/shard_map/reduce_sum | solution.py:163
  474.7 9.2 %gather_fusion.3 = bf16[2048,512]{1,0:T(8,128)(2,1)} fusion(bf16[2561,512]{1,0:T(8,128)(2,1)S(1)} %concatenate.37, s32[2048]{0:T(1024)S(1)} %broadcast_clamp_fusion.1), kind=kCustom, calls=%fused_computation.3 | custom fusion | bytes 4202496 | tf_op jit(solution)/shard_map/gather | solution.py:162
  486.9 6.7 %reduce_sum.48 = bf16[1024,512]{1,0:T(8,128)(2,1)} reduce(bf16[1024,2,512]{2,1,0:T(2,128)(2,1)S(1)} %reshape.427, bf16[]{:T(256)} %constant.73.clone.1), dimensions={1}, to_apply=%region_4.5 | reduce | flops 524288 | bytes 3145730 | tf_op jit(solution)/shard_map/reduce_sum | solution.py:163
  (98 shorter events, 54.4 us)
Async XLA Ops:
  8.9 11.8 %all-to-all-start.3 = ((bf16[4,8,5376]{2,1,0:T(8,128)(2,1)}), bf16[4,8,5376]{2,1,0:T(8,128)(2,1)S(1)}, u32[]{:S(2)}, u32[]{:S(2)}) async-start(bf16[4,8,5376]{2,1,0:T(8,128)(2,1)} %pad_maximum_fusion.1), calls=%async_computation.3 | async-start | bytes 688128 | tf_op jit(solution)/shard_map/all_to_all | solution.py:136
  13.4 168.3 %all-gather.2.cloned.1.call-start = ((), (), s32[]{:S(2)}) async-start(), calls=%async_computation.13 | async-start | bytes 5849088 | tf_op jit(solution)/shard_map/all_gather | solution.py:137
  20.7 0.7 copy-start.4
  44.1 30.4 %all-to-all-start.2 = ((f32[8,1,320]{2,1,0:T(1,128)}), f32[8,1,320]{2,1,0:T(1,128)S(1)}, u32[]{:S(2)}, u32[]{:S(2)}) async-start(f32[8,1,320]{2,1,0:T(1,128)} %all_to_all.50), calls=%async_computation.2 | async-start | bytes 24576 | tf_op jit(solution)/shard_map/all_to_all | solution.py:153
  74.5 14.8 %all-to-all-start.7 = ((f32[8,1,320]{2,1,0:T(1,128)}), f32[8,1,320]{2,1,0:T(1,128)S(1)}, u32[]{:S(2)}, u32[]{:S(2)}) async-start(f32[8,1,320]{2,1,0:T(1,128)} %all_to_all.56), calls=%async_computation.7 | async-start | bytes 24576 | tf_op jit(solution)/shard_map/all_to_all | solution.py:153
  89.3 37.6 %all-to-all-start.5 = ((bf16[8,320,512]{2,1,0:T(8,128)(2,1)}), bf16[8,320,512]{2,1,0:T(8,128)(2,1)}, u32[]{:S(2)}, u32[]{:S(2)}) async-start(bf16[8,320,512]{2,1,0:T(8,128)(2,1)} %bitcast.74), calls=%async_computation.5 | async-start | bytes 5242880 | tf_op jit(solution)/shard_map/all_to_all | solution.py:151
  126.9 37.1 %all-to-all-start = ((bf16[8,320,512]{2,1,0:T(8,128)(2,1)}), bf16[8,320,512]{2,1,0:T(8,128)(2,1)}, u32[]{:S(2)}, u32[]{:S(2)}) async-start(bf16[8,320,512]{2,1,0:T(8,128)(2,1)} %bitcast.73), calls=%async_computation | async-start | bytes 5242880 | tf_op jit(solution)/shard_map/all_to_all | solution.py:151
  164.0 37.6 %all-to-all-start.1 = ((bf16[8,320,512]{2,1,0:T(8,128)(2,1)}), bf16[8,320,512]{2,1,0:T(8,128)(2,1)}, u32[]{:S(2)}, u32[]{:S(2)}) async-start(bf16[8,320,512]{2,1,0:T(8,128)(2,1)} %bitcast.72), calls=%async_computation.1 | async-start | bytes 5242880 | tf_op jit(solution)/shard_map/all_to_all | solution.py:152
  201.6 62.8 %all-to-all-start.6 = ((bf16[8,320,512]{2,1,0:T(8,128)(2,1)}), bf16[8,320,512]{2,1,0:T(8,128)(2,1)S(1)}, u32[]{:S(2)}, u32[]{:S(2)}) async-start(bf16[8,320,512]{2,1,0:T(8,128)(2,1)} %bitcast.22), calls=%async_computation.6 | async-start | bytes 5242880 | tf_op jit(solution)/shard_map/all_to_all | solution.py:152
  205.2 216.8 %reduce-scatter.2.cloned.1.call-start = ((), (), s32[]{:S(2)}) async-start(), calls=%async_computation.14 | async-start | bytes 11698176 | tf_op jit(solution)/shard_map/reduce_scatter | solution.py:165
  264.4 1.5 copy-start.3
  328.1 20.1 %copy-start.2 = (bf16[2560,512]{1,0:T(8,128)(2,1)S(1)}, bf16[2560,512]{1,0:T(8,128)(2,1)}, u32[]{:S(2)}) copy-start(bf16[2560,512]{1,0:T(8,128)(2,1)} %get-tuple-element.13) | copy-start | bytes 7864324
  330.7 9.8 %all-to-all-start.10 = ((f32[8,1,320]{2,1,0:T(1,128)}), f32[8,1,320]{2,1,0:T(1,128)S(1)}, u32[]{:S(2)}, u32[]{:S(2)}) async-start(f32[8,1,320]{2,1,0:T(1,128)} %all_to_all.65), calls=%async_computation.10 | async-start | bytes 24576 | tf_op jit(solution)/shard_map/all_to_all | solution.py:161
  384.1 36.4 %all-to-all-start.4 = ((bf16[8,320,512]{2,1,0:T(8,128)(2,1)}), bf16[8,320,512]{2,1,0:T(8,128)(2,1)S(1)}, u32[]{:S(2)}, u32[]{:S(2)}) async-start(bf16[8,320,512]{2,1,0:T(8,128)(2,1)} %bitcast.81), calls=%async_computation.4 | async-start | bytes 5242880 | tf_op jit(solution)/shard_map/all_to_all | solution.py:160
  420.5 6.2 %copy-start = (bf16[8,320,512]{2,1,0:T(8,128)(2,1)}, bf16[8,320,512]{2,1,0:T(8,128)(2,1)S(1)}, u32[]{:S(2)}) copy-start(bf16[8,320,512]{2,1,0:T(8,128)(2,1)S(1)} %all-to-all-done.4) | copy-start | bytes 7864324
  422.0 74.3 %all-to-all-start.11 = ((f32[4,8,5376]{2,1,0:T(8,128)}), f32[4,8,5376]{2,1,0:T(8,128)}, u32[]{:S(2)}, u32[]{:S(2)}) async-start(f32[4,8,5376]{2,1,0:T(8,128)} %bitcast.85), calls=%async_computation.12 | async-start | bytes 1376256 | tf_op jit(solution)/shard_map/all_to_all | solution.py:166
  486.9 6.7 %copy-start.1 = (bf16[1024,512]{1,0:T(8,128)(2,1)S(1)}, bf16[1024,512]{1,0:T(8,128)(2,1)}, u32[]{:S(2)}) copy-start(bf16[1024,512]{1,0:T(8,128)(2,1)} %reduce_sum.51) | copy-start | bytes 3145732
Sparse Core Ops, SparseCore 0:
  21.6 59.2 all-gather.1
  328.2 93.7 reduce-scatter.1
